TPU v7x, 1024 devices: a whole 4x8x16 slice. The times are simulated.
1024 devices in a mesh: replica: 64 (over z_hi, y, core), shard: 16 (over x, z_lo).
Axes of the slice: x: 4, y: 8, z: 16 (z_hi: 4, z_lo: 4; z = z_hi * 4 + z_lo), core: 2. Of those that a mesh axis runs over, the one named last changes fastest.
Arguments:
- deltas: bfloat16 [64, 4194304], P('replica', 'shard'), may hold values from -16 to 16
- counts: int32 [32], replicated, may hold values from 1000 to 8999, as said below
- momentum: float32 [8388608], P(('shard', 'replica')), may hold values from -4 to 4
- params: bfloat16 [8388608], P(('shard', 'replica')), may hold values from -6 to 6
Outputs:
- new_momentum: float32 [8388608], P(('shard', 'replica'))
- new_params: bfloat16 [8388608], P('shard')
Inputs may be any that keep to these rules, and one draw needn't show every extreme that they name: `counts`: tokens processed by each worker.
All inputs are finite; a program needn't handle non-finite values.
Results may differ from a plain program's by a relative error of at most 0.001.
Values may be sent and summed in bfloat16 or wider, within the bound.
No kernel may reach another device: no remote copies, remote signals or barrier semaphores. Data moves between devices by JAX's collectives and lax.ppermute only.
A program may use at most 32 MiB of HBM per device.

v0:
```python
import jax
import jax.numpy as jnp
from jax import lax
from jax.experimental import pallas as pl
from jax.experimental.pallas import tpu as pltpu
from jax.sharding import Mesh
from jax.sharding import PartitionSpec as P

momentum_rate = 0.9
outer_rate = 0.7
READS = 4

VMEM = pl.BlockSpec(memory_space=pltpu.VMEM)
SMEM = pl.BlockSpec(memory_space=pltpu.SMEM)
HBM = pl.BlockSpec(memory_space=pltpu.HBM)


def on_chip(x):
    return pltpu.with_memory_space_constraint(x, pltpu.VMEM)


def prepared(deltas, counts, momentum, params, z, ny, nc, nz):
    rows = momentum.shape[0]
    pairs, planes = ny * nc, nz // nc
    step = deltas.shape[1] // READS
    pieces_of = step // (rows * 128)
    workers = counts.shape[0]

    def body(z_ref, counts_ref, src, old, was, out, shares_ref, old_ref, was_ref, held, sems):
        reads = [
            pltpu.make_async_copy(
                src.at[:, pl.ds(k * step, step)], held.at[:, pl.ds(k * step, step)], sems.at[k]
            )
            for k in range(READS)
        ]
        for read in reads:
            read.start()
        rest = [
            pltpu.make_async_copy(old, old_ref, sems.at[READS]),
            pltpu.make_async_copy(was, was_ref, sems.at[READS + 1]),
        ]
        for read in rest:
            read.start()
        total = counts_ref[0]
        for w in range(1, workers):
            total += counts_ref[w]
        whole = jnp.full((8, 128), total, jnp.int32).astype(jnp.float32)
        first = z_ref[0] * ny
        for y in range(ny):
            count = jnp.full((8, 128), counts_ref[first + y], jnp.int32).astype(jnp.float32)
            shares_ref[y] = count / whole
        for k, read in enumerate(reads):
            read.wait()
            for piece in range(k * pieces_of, (k + 1) * pieces_of):
                at = piece * rows * 128
                block = held[:, at : at + rows * 128].astype(jnp.float32).reshape(rows, 128)
                out[piece % pairs, piece // pairs] = block.astype(jnp.bfloat16)
        for read in rest:
            read.wait()

    return pl.pallas_call(
        body,
        out_shape=[
            pltpu.VMEM((pairs, planes, rows, 128), jnp.bfloat16),
            pltpu.VMEM((ny, 8, 128), jnp.float32),
            pltpu.VMEM((rows, 128), momentum.dtype),
            pltpu.VMEM((rows, 128), params.dtype),
        ],
        in_specs=[SMEM, SMEM, HBM, HBM, HBM],
        out_specs=[VMEM] * 4,
        scratch_shapes=[
            pltpu.VMEM(deltas.shape, deltas.dtype),
            pltpu.SemaphoreType.DMA((READS + 2,)),
        ],
        name="prepared",
    )(z.reshape(1), counts, deltas, momentum, params)


def weighted(got, shares, nc):
    pairs, planes, rows, _ = got.shape

    def body(shares_ref, got_ref, out_ref):
        shares = [shares_ref[y][None] for y in range(pairs // nc)]
        for h in range(nc):
            for p in range(planes):
                acc = None
                for y, share in enumerate(shares):
                    term = got_ref[y * nc + h, p].astype(jnp.float32).reshape(rows // 8, 8, 128)
                    term = share * term
                    acc = term if acc is None else acc + term
                out_ref[h * planes + p] = acc.reshape(rows, 128)

    return pl.pallas_call(
        body,
        out_shape=pltpu.VMEM((nc * planes, rows, 128), jnp.float32),
        in_specs=[VMEM, VMEM],
        out_specs=VMEM,
        name="weighted",
    )(on_chip(shares), on_chip(got))


def updated(got, old, was):
    planes, rows, _ = got.shape

    def body(got_ref, old_ref, was_ref, momentum_ref, out_ref):
        grad = got_ref[0]
        for z in range(1, planes):
            grad = grad + got_ref[z]
        m = momentum_rate * old_ref[...] + grad
        momentum_ref[...] = m
        new = was_ref[...].astype(jnp.float32) - outer_rate * (grad + momentum_rate * m)
        new = new.astype(jnp.bfloat16)
        for z in range(planes):
            out_ref[z] = new

    return pl.pallas_call(
        body,
        out_shape=[
            pltpu.VMEM((rows, 128), jnp.float32),
            pltpu.VMEM((planes, rows, 128), jnp.bfloat16),
        ],
        in_specs=[VMEM] * 3,
        out_specs=[VMEM] * 2,
        name="updated",
    )(on_chip(got), on_chip(old), on_chip(was))


def exchanged(x, axes):
    return lax.all_to_all(x, axes, 0, 0, tiled=True)


def local(deltas, counts, momentum, params):
    nz, ny, nc = lax.axis_size("z"), lax.axis_size("y"), lax.axis_size("c")
    z, c = lax.axis_index("z"), lax.axis_index("c")
    rows = momentum.shape[0] // 128

    pieces, shares, old, was = prepared(
        deltas, counts, momentum.reshape(rows, 128), params.reshape(rows, 128), z, ny, nc, nz
    )
    partial = weighted(exchanged(pieces, ("y", "c")), shares, nc)
    new_momentum, copies = updated(exchanged(partial, "z"), old, was)
    plane = exchanged(copies, "z")
    own = exchanged(jnp.broadcast_to(plane[None], (ny, *plane.shape)), "y")
    other = lax.ppermute(own, "c", [(0, 1), (1, 0)])

    out = jnp.zeros((nz, ny, nc, rows, 128), jnp.bfloat16)
    for at, half in ((c, own), (1 - c, other)):
        block = jnp.swapaxes(half, 0, 1)[:, :, None]
        out = lax.dynamic_update_slice(out, block, (0, 0, at, 0, 0))
    return new_momentum.reshape(-1), out.reshape(-1)


def solution(mesh):
    torus = Mesh(mesh.devices.reshape(4, 8, 2, mesh.shape["shard"]), ("z", "y", "c", "shard"))
    R = ("z", "y", "c")
    return jax.shard_map(
        local,
        mesh=torus,
        in_specs=(P(R, "shard"), P(), P(("shard",) + R), P(("shard",) + R)),
        out_specs=(P(("shard",) + R), P("shard")),
        check_vma=False,
    )
```

profile of v0, /device:TPU:1, one launch (start us, length us, event | category | flops | bytes accessed | tf_op | source)
XLA Modules:
  0.0 103.6 jit_solution(10183215450989835689)
XLA Ops:
  0.6 2.0 %prepared.1 = (bf16[16,2,64,128]{3,2,1,0:T(8,128)(2,1)S(1)}, f32[8,8,128]{2,1,0:T(8,128)S(1)}, f32[64,128]{1,0:T(8,128)S(1)}, bf16[64,128]{1,0:T(8,128)(2,1)S(1)}) custom-call(s32[1]{0:T(128)} %bitcast.z_ref, s32[32]{0:T(128)} %counts_ref.1, bf16[1,262144]{1,0:T(2,128)(2,1)} %src.1, f32[64,128]{1,0:T(8,128)} %bitcast.15, bf16[64,128]{1,0:T(8,128)(2,1)} %bitcast.16), custom_call_target="tpu_custom_call" | custom-call | tf_op jit(solution)/shard_map/prepared/pallas_call | solution.py:61
  2.6 33.9 %all_to_all.20.got_ref = bf16[16,2,64,128]{3,2,1,0:T(8,128)(2,1)S(1)} all-to-all(bf16[16,2,64,128]{3,2,1,0:T(8,128)(2,1)S(1)} %get-tuple-element.9), channel_id=1, replica_groups=mesh['z'=4,'y'=8,'c'=2,'shard'=16] {'y','c'}, dimensions={0} | all-to-all | bytes 1048576 | tf_op jit(solution)/shard_map/all_to_all | solution.py:129
  36.5 0.1 weighted.1
  36.6 26.5 %all_to_all.21.got_ref = f32[4,64,128]{2,1,0:T(8,128)S(1)} all-to-all(f32[4,64,128]{2,1,0:T(8,128)S(1)} %weighted.1), channel_id=1, replica_groups=mesh['z'=4,'y'=8,'c'=2,'shard'=16] {'z'}, dimensions={0} | all-to-all | bytes 262144 | tf_op jit(solution)/shard_map/all_to_all | solution.py:129
  63.1 15.0 %all_to_all.22 = bf16[4,64,128]{2,1,0:T(8,128)(2,1)S(1)} all-to-all(bf16[4,64,128]{2,1,0:T(8,128)(2,1)S(1)} %get-tuple-element.13), channel_id=1, replica_groups=mesh['z'=4,'y'=8,'c'=2,'shard'=16] {'z'}, dimensions={0} | all-to-all | bytes 131072 | tf_op jit(solution)/shard_map/all_to_all | solution.py:129
  78.1 0.1 broadcast_in_dim.16
  78.2 17.7 %all_to_all.23 = bf16[8,4,64,128]{3,2,1,0:T(8,128)(2,1)S(1)} all-to-all(bf16[8,4,64,128]{3,2,1,0:T(8,128)(2,1)S(1)} %broadcast_in_dim.16), channel_id=1, replica_groups=mesh['z'=4,'y'=8,'c'=2,'shard'=16] {'y'}, dimensions={0} | all-to-all | bytes 1048576 | tf_op jit(solution)/shard_map/all_to_all | solution.py:129
  96.0 5.0 %collective-permute-start = (bf16[8,4,64,128]{3,2,0,1:T(8,128)(2,1)S(1)}, bf16[8,4,64,128]{3,2,0,1:T(8,128)(2,1)S(1)}, u32[]{:S(2)}, u32[]{:S(2)}) collective-permute-start(bf16[8,4,64,128]{3,2,0,1:T(8,128)(2,1)S(1)} %copy.7), channel_id=1, source_target_pairs={{0,16},{16,0},{1,17},{17,1},{2,18},{18,2},{3,19},{19,3},{4,20},{20... | collective-permute-start | bytes 1572872 | tf_op jit(solution)/shard_map/ppermute | solution.py:144
  101.0 0.6 copy.12
  101.7 0.2 broadcast_in_dim.15
  101.9 0.1 bitcast_dynamic-update-slice_fusion.1
  102.0 0.6 collective-permute-done
  102.5 0.1 bitcast_dynamic-update-slice_fusion
  102.6 0.0 copy-start
  102.6 1.0 copy-done
  (2 shorter events, 0.1 us)
Async XLA Ops:
  96.0 6.5 %collective-permute-start = (bf16[8,4,64,128]{3,2,0,1:T(8,128)(2,1)S(1)}, bf16[8,4,64,128]{3,2,0,1:T(8,128)(2,1)S(1)}, u32[]{:S(2)}, u32[]{:S(2)}) collective-permute-start(bf16[8,4,64,128]{3,2,0,1:T(8,128)(2,1)S(1)} %copy.7), channel_id=1, source_target_pairs={{0,16},{16,0},{1,17},{17,1},{2,18},{18,2},{3,19},{19,3},{4,20},{20... | collective-permute-start | bytes 1572872 | tf_op jit(solution)/shard_map/ppermute | solution.py:144
  102.6 1.0 copy-start
where the time goes:
time: 104 us
  blocking collectives  93.1 us (90%)
  starting transfers between devices  5.02 us (5%)
  local copies, waits for them, and re-layouts  2.11 us (2%)
  Pallas kernels  2.08 us (2%)
    all_to_all x4, blocking collectives, exchanged(): return lax.all_to_all(x, axes, 0, 0, tiled=True)  93.1 us
    ppermute x1, starting transfers between devices, local(): other = lax.ppermute(own, 'c', [(0, 1), (1, 0)])  5.02 us
  transfers between devices with their start and end apart: 1, of which 1 were waited for; matrix products, arithmetic and copies ran while one was open for 1% of the time, Pallas kernels for 0%

commit v1 on v0

--- a/solution.py
+++ b/solution.py
@@ -8,6 +8,8 @@
 
 momentum_rate = 0.9
 outer_rate = 0.7
+grad_rate = outer_rate * (1 + momentum_rate)
+old_rate = outer_rate * momentum_rate * momentum_rate
 READS = 4
 
 VMEM = pl.BlockSpec(memory_space=pltpu.VMEM)
@@ -76,10 +78,10 @@
     )(z.reshape(1), counts, deltas, momentum, params)
 
 
-def weighted(got, shares, nc):
+def weighted(got, shares, old, was, z, nc):
     pairs, planes, rows, _ = got.shape
 
-    def body(shares_ref, got_ref, out_ref):
+    def body(z_ref, shares_ref, got_ref, old_ref, was_ref, out_ref, own_ref):
         shares = [shares_ref[y][None] for y in range(pairs // nc)]
         for h in range(nc):
             for p in range(planes):
@@ -89,29 +91,38 @@
                     term = share * term
                     acc = term if acc is None else acc + term
                 out_ref[h * planes + p] = acc.reshape(rows, 128)
+        z = z_ref[0]
+        own = out_ref[z]
+        own_ref[...] = own
+        rest = was_ref[...].astype(jnp.float32) * (1 / grad_rate) - old_ref[...] * (old_rate / grad_rate)
+        out_ref[z] = own - rest
 
     return pl.pallas_call(
         body,
-        out_shape=pltpu.VMEM((nc * planes, rows, 128), jnp.float32),
-        in_specs=[VMEM, VMEM],
-        out_specs=VMEM,
+        out_shape=[
+            pltpu.VMEM((nc * planes, rows, 128), jnp.float32),
+            pltpu.VMEM((rows, 128), jnp.float32),
+        ],
+        in_specs=[SMEM] + [VMEM] * 4,
+        out_specs=[VMEM] * 2,
         name="weighted",
-    )(on_chip(shares), on_chip(got))
+    )(z.reshape(1), *map(on_chip, (shares, got, old, was)))
 
 
-def updated(got, old, was):
-    planes, rows, _ = got.shape
+def updated(every, own, old, z):
+    planes, _, rows, _ = every.shape
 
-    def body(got_ref, old_ref, was_ref, momentum_ref, out_ref):
-        grad = got_ref[0]
-        for z in range(1, planes):
-            grad = grad + got_ref[z]
-        m = momentum_rate * old_ref[...] + grad
-        momentum_ref[...] = m
-        new = was_ref[...].astype(jnp.float32) - outer_rate * (grad + momentum_rate * m)
-        new = new.astype(jnp.bfloat16)
-        for z in range(planes):
-            out_ref[z] = new
+    def body(z_ref, every_ref, own_ref, old_ref, momentum_ref, out_ref):
+        z = z_ref[0]
+        grad = own_ref[...]
+        for step in range(1, planes):
+            grad = grad + every_ref[(z + step) % planes, z]
+        momentum_ref[...] = momentum_rate * old_ref[...] + grad
+        for p in range(planes):
+            total = every_ref[0, p]
+            for k in range(1, planes):
+                total = total + every_ref[k, p]
+            out_ref[p] = (-grad_rate * total).astype(jnp.bfloat16)
 
     return pl.pallas_call(
         body,
@@ -119,10 +130,10 @@
             pltpu.VMEM((rows, 128), jnp.float32),
             pltpu.VMEM((planes, rows, 128), jnp.bfloat16),
         ],
-        in_specs=[VMEM] * 3,
+        in_specs=[SMEM] + [VMEM] * 3,
         out_specs=[VMEM] * 2,
         name="updated",
-    )(on_chip(got), on_chip(old), on_chip(was))
+    )(z.reshape(1), *map(on_chip, (every, own, old)))
 
 
 def exchanged(x, axes):
@@ -137,9 +148,8 @@
     pieces, shares, old, was = prepared(
         deltas, counts, momentum.reshape(rows, 128), params.reshape(rows, 128), z, ny, nc, nz
     )
-    partial = weighted(exchanged(pieces, ("y", "c")), shares, nc)
-    new_momentum, copies = updated(exchanged(partial, "z"), old, was)
-    plane = exchanged(copies, "z")
+    partial, mine = weighted(exchanged(pieces, ("y", "c")), shares, old, was, z, nc)
+    new_momentum, plane = updated(lax.all_gather(partial, "z"), mine, old, z)
     own = exchanged(jnp.broadcast_to(plane[None], (ny, *plane.shape)), "y")
     other = lax.ppermute(own, "c", [(0, 1), (1, 0)])
 

time: 104 us -> 90.8 us (0.87)
  blocking collectives: 93.1 us -> 80.3 us
    all_to_all x4 -> x2, blocking collectives: 93.1 us -> 52.5 us  [exchanged(): return lax.all_to_all(x, axes, 0, 0, tiled=True)]
    all_gather x0 -> x1, blocking collectives: none -> 27.8 us  [local(): new_momentum, plane = updated(lax.all_gather(partial, 'z'), mine, old, z)]
where the time goes in v1:
time: 90.8 us; the launch traced here: 89.9 us
  blocking collectives  80.3 us (88%)
  starting transfers between devices  4.17 us (5%)
  local copies, waits for them, and re-layouts  2.11 us (2%)
  Pallas kernels  2.1 us (2%)
    all_to_all x2, blocking collectives, exchanged(): return lax.all_to_all(x, axes, 0, 0, tiled=True)  52.5 us
    all_gather x1, blocking collectives, local(): new_momentum, plane = updated(lax.all_gather(partial, 'z'), mine, old, z)  27.8 us
    ppermute x1, starting transfers between devices, local(): other = lax.ppermute(own, 'c', [(0, 1), (1, 0)])  4.17 us
    pallas_call x1, Pallas kernels, prepared(): pl.pallas_call(body, out_shape=[pltpu.VMEM((pairs, planes, rows, 128), jn...  1.96 us
  transfers between devices with their start and end apart: 1, of which 1 were waited for; matrix products, arithmetic and copies ran while one was open for 1% of the time, Pallas kernels for 0%

profile of v1, /device:TPU:1, one launch (start us, length us, event | category | flops | bytes accessed | tf_op | source)
XLA Modules:
  0.0 89.9 jit_solution(15625733434054717156)
XLA Ops:
  0.6 2.0 %prepared.1 = (bf16[16,2,64,128]{3,2,1,0:T(8,128)(2,1)S(1)}, f32[8,8,128]{2,1,0:T(8,128)S(1)}, f32[64,128]{1,0:T(8,128)S(1)}, bf16[64,128]{1,0:T(8,128)(2,1)S(1)}) custom-call(s32[1]{0:T(128)} %bitcast.z_ref, s32[32]{0:T(128)} %counts_ref.1, bf16[1,262144]{1,0:T(2,128)(2,1)} %src.1, f32[64,128]{1,0:T(8,128)} %bitcast.17, bf16[64,128]{1,0:T(8,128)(2,1)} %bitcast.18), custom_call_target="tpu_custom_call" | custom-call | tf_op jit(solution)/shard_map/prepared/pallas_call | solution.py:63
  2.6 33.9 %all_to_all.10.got_ref = bf16[16,2,64,128]{3,2,1,0:T(8,128)(2,1)S(1)} all-to-all(bf16[16,2,64,128]{3,2,1,0:T(8,128)(2,1)S(1)} %get-tuple-element.11), channel_id=1, replica_groups=mesh['z'=4,'y'=8,'c'=2,'shard'=16] {'y','c'}, dimensions={0} | all-to-all | bytes 1048576 | tf_op jit(solution)/shard_map/all_to_all | solution.py:140
  36.5 0.1 weighted.1
  36.6 27.8 %all-gather = f32[16,64,128]{2,1,0:T(8,128)S(1)} all-gather(f32[4,64,128]{2,1,0:T(8,128)S(1)} %get-tuple-element.14), channel_id=2, replica_groups=mesh['z'=4,'y'=8,'c'=2,'shard'=16] {'z'}, dimensions={0}, use_global_device_ids=true | all-gather | bytes 655360 | tf_op jit(solution)/shard_map/all_gather | solution.py:152
  64.4 0.1 broadcast_in_dim.16
  64.5 18.6 %all_to_all.11 = bf16[8,4,64,128]{3,2,1,0:T(8,128)(2,1)S(1)} all-to-all(bf16[8,4,64,128]{3,2,1,0:T(8,128)(2,1)S(1)} %broadcast_in_dim.16), channel_id=1, replica_groups=mesh['z'=4,'y'=8,'c'=2,'shard'=16] {'y'}, dimensions={0} | all-to-all | bytes 1048576 | tf_op jit(solution)/shard_map/all_to_all | solution.py:140
  83.2 4.2 %collective-permute-start = (bf16[8,4,64,128]{3,2,0,1:T(8,128)(2,1)S(1)}, bf16[8,4,64,128]{3,2,0,1:T(8,128)(2,1)S(1)}, u32[]{:S(2)}, u32[]{:S(2)}) collective-permute-start(bf16[8,4,64,128]{3,2,0,1:T(8,128)(2,1)S(1)} %copy.7), channel_id=1, source_target_pairs={{0,16},{16,0},{1,17},{17,1},{2,18},{18,2},{3,19},{19,3},{4,20},{20... | collective-permute-start | bytes 1572872 | tf_op jit(solution)/shard_map/ppermute | solution.py:154
  87.3 0.6 copy.12
  88.0 0.2 broadcast_in_dim.15
  88.2 0.1 bitcast_dynamic-update-slice_fusion.1
  88.3 0.6 collective-permute-done
  88.9 0.1 bitcast_dynamic-update-slice_fusion
  88.9 0.0 copy-start
  88.9 1.0 %copy-done = bf16[4,8,2,64,128]{4,3,2,1,0:T(8,128)(2,1)} copy-done((bf16[4,8,2,64,128]{4,3,2,1,0:T(8,128)(2,1)}, bf16[4,8,2,64,128]{4,3,2,1,0:T(8,128)(2,1)S(1)}, u32[]{:S(2)}) %copy-start) | copy-done | bytes 1048600
  (2 shorter events, 0.1 us)
Async XLA Ops:
  83.2 5.7 %collective-permute-start = (bf16[8,4,64,128]{3,2,0,1:T(8,128)(2,1)S(1)}, bf16[8,4,64,128]{3,2,0,1:T(8,128)(2,1)S(1)}, u32[]{:S(2)}, u32[]{:S(2)}) collective-permute-start(bf16[8,4,64,128]{3,2,0,1:T(8,128)(2,1)S(1)} %copy.7), channel_id=1, source_target_pairs={{0,16},{16,0},{1,17},{17,1},{2,18},{18,2},{3,19},{19,3},{4,20},{20... | collective-permute-start | bytes 1572872 | tf_op jit(solution)/shard_map/ppermute | solution.py:154
  88.9 1.0 %copy-start = (bf16[4,8,2,64,128]{4,3,2,1,0:T(8,128)(2,1)}, bf16[4,8,2,64,128]{4,3,2,1,0:T(8,128)(2,1)S(1)}, u32[]{:S(2)}) copy-start(bf16[4,8,2,64,128]{4,3,2,1,0:T(8,128)(2,1)S(1)} %bitcast_dynamic-update-slice_fusion) | copy-start | bytes 3145732

commit v2 on v1

--- a/solution.py
+++ b/solution.py
@@ -11,6 +11,10 @@
 grad_rate = outer_rate * (1 + momentum_rate)
 old_rate = outer_rate * momentum_rate * momentum_rate
 READS = 4
+Y_ORDER = (0, 4, 2, 6, 1, 5, 3, 7)
+CORES = 2
+ALL_ORDER = [y * CORES + c for c in range(CORES) for y in Y_ORDER]
+SAME_CORE = [[y * CORES + c for y in Y_ORDER] for c in range(CORES)]
 
 VMEM = pl.BlockSpec(memory_space=pltpu.VMEM)
 SMEM = pl.BlockSpec(memory_space=pltpu.SMEM)
@@ -28,7 +32,7 @@
     pieces_of = step // (rows * 128)
     workers = counts.shape[0]
 
-    def body(z_ref, counts_ref, src, old, was, out, shares_ref, old_ref, was_ref, held, sems):
+    def body(z_ref, counts, src, old, was, out, shares_ref, old_ref, was_ref, held, counts_ref, sems):
         reads = [
             pltpu.make_async_copy(
                 src.at[:, pl.ds(k * step, step)], held.at[:, pl.ds(k * step, step)], sems.at[k]
@@ -37,12 +41,15 @@
         ]
         for read in reads:
             read.start()
+        tokens = pltpu.make_async_copy(counts, counts_ref, sems.at[READS + 2])
+        tokens.start()
         rest = [
             pltpu.make_async_copy(old, old_ref, sems.at[READS]),
             pltpu.make_async_copy(was, was_ref, sems.at[READS + 1]),
         ]
         for read in rest:
             read.start()
+        tokens.wait()
         total = counts_ref[0]
         for w in range(1, workers):
             total += counts_ref[w]
@@ -56,7 +63,7 @@
             for piece in range(k * pieces_of, (k + 1) * pieces_of):
                 at = piece * rows * 128
                 block = held[:, at : at + rows * 128].astype(jnp.float32).reshape(rows, 128)
-                out[piece % pairs, piece // pairs] = block.astype(jnp.bfloat16)
+                out[ALL_ORDER.index(piece % pairs), piece // pairs] = block.astype(jnp.bfloat16)
         for read in rest:
             read.wait()
 
@@ -68,11 +75,12 @@
             pltpu.VMEM((rows, 128), momentum.dtype),
             pltpu.VMEM((rows, 128), params.dtype),
         ],
-        in_specs=[SMEM, SMEM, HBM, HBM, HBM],
+        in_specs=[SMEM, HBM, HBM, HBM, HBM],
         out_specs=[VMEM] * 4,
         scratch_shapes=[
             pltpu.VMEM(deltas.shape, deltas.dtype),
-            pltpu.SemaphoreType.DMA((READS + 2,)),
+            pltpu.SMEM(counts.shape, counts.dtype),
+            pltpu.SemaphoreType.DMA((READS + 3,)),
         ],
         name="prepared",
     )(z.reshape(1), counts, deltas, momentum, params)
@@ -87,7 +95,7 @@
             for p in range(planes):
                 acc = None
                 for y, share in enumerate(shares):
-                    term = got_ref[y * nc + h, p].astype(jnp.float32).reshape(rows // 8, 8, 128)
+                    term = got_ref[ALL_ORDER.index(y * nc + h), p].astype(jnp.float32).reshape(rows // 8, 8, 128)
                     term = share * term
                     acc = term if acc is None else acc + term
                 out_ref[h * planes + p] = acc.reshape(rows, 128)
@@ -136,33 +144,35 @@
     )(z.reshape(1), *map(on_chip, (every, own, old)))
 
 
-def exchanged(x, axes):
-    return lax.all_to_all(x, axes, 0, 0, tiled=True)
+def exchanged(x, groups):
+    return lax.all_to_all(x, "yc", 0, 0, tiled=True, axis_index_groups=groups)
 
 
 def local(deltas, counts, momentum, params):
-    nz, ny, nc = lax.axis_size("z"), lax.axis_size("y"), lax.axis_size("c")
-    z, c = lax.axis_index("z"), lax.axis_index("c")
+    nz, nc = lax.axis_size("z"), CORES
+    ny = lax.axis_size("yc") // nc
+    z, c = lax.axis_index("z"), lax.axis_index("yc") % nc
     rows = momentum.shape[0] // 128
 
     pieces, shares, old, was = prepared(
         deltas, counts, momentum.reshape(rows, 128), params.reshape(rows, 128), z, ny, nc, nz
     )
-    partial, mine = weighted(exchanged(pieces, ("y", "c")), shares, old, was, z, nc)
+    partial, mine = weighted(exchanged(pieces, [ALL_ORDER]), shares, old, was, z, nc)
     new_momentum, plane = updated(lax.all_gather(partial, "z"), mine, old, z)
-    own = exchanged(jnp.broadcast_to(plane[None], (ny, *plane.shape)), "y")
-    other = lax.ppermute(own, "c", [(0, 1), (1, 0)])
+    own = exchanged(jnp.broadcast_to(plane[None], (ny, *plane.shape)), SAME_CORE)
+    other = lax.ppermute(own, "yc", [(i, i ^ 1) for i in range(ny * nc)])
 
     out = jnp.zeros((nz, ny, nc, rows, 128), jnp.bfloat16)
     for at, half in ((c, own), (1 - c, other)):
-        block = jnp.swapaxes(half, 0, 1)[:, :, None]
+        bits = half.reshape(2, 2, 2, nz, rows, 128)
+        block = jnp.transpose(bits, (3, 2, 1, 0, 4, 5)).reshape(nz, ny, 1, rows, 128)
         out = lax.dynamic_update_slice(out, block, (0, 0, at, 0, 0))
     return new_momentum.reshape(-1), out.reshape(-1)
 
 
 def solution(mesh):
-    torus = Mesh(mesh.devices.reshape(4, 8, 2, mesh.shape["shard"]), ("z", "y", "c", "shard"))
-    R = ("z", "y", "c")
+    torus = Mesh(mesh.devices.reshape(4, 16, mesh.shape["shard"]), ("z", "yc", "shard"))
+    R = ("z", "yc")
     return jax.shard_map(
         local,
         mesh=torus,

time: 90.8 us -> 87.7 us (0.966)
  blocking collectives: 80.3 us -> 73.6 us
  starting transfers between devices: 4.17 us -> 7.92 us
    all_to_all x2, blocking collectives: 52.5 us -> 47.6 us  [exchanged(): return lax.all_to_all(x, 'yc', 0, 0, tiled=True, axis_index_groups=groups)]
    ppermute x1, starting transfers between devices: 4.17 us -> 7.92 us  [local(): other = lax.ppermute(own, 'yc', [(i, i ^ 1) for i in range(ny * nc)])]
    all_gather x1, blocking collectives: 27.8 us -> 26 us  [local(): new_momentum, plane = updated(lax.all_gather(partial, 'z'), mine, old, z)]
where the time goes in v2:
time: 87.7 us; the launch traced here: 86.4 us
  blocking collectives  73.6 us (84%)
  starting transfers between devices  7.92 us (9%)
  local copies, waits for them, and re-layouts  2.15 us (2%)
  Pallas kernels  1.45 us (2%)
    all_to_all x2, blocking collectives, exchanged(): return lax.all_to_all(x, 'yc', 0, 0, tiled=True, axis_index_groups=groups)  47.6 us
    all_gather x1, blocking collectives, local(): new_momentum, plane = updated(lax.all_gather(partial, 'z'), mine, old, z)  26 us
    ppermute x1, starting transfers between devices, local(): other = lax.ppermute(own, 'yc', [(i, i ^ 1) for i in range(ny * nc)])  7.92 us
  transfers between devices with their start and end apart: 1, of which 1 were waited for; matrix products, arithmetic and copies ran while one was open for 1% of the time, Pallas kernels for 0%

profile of v2, /device:TPU:1, one launch (start us, length us, event | category | flops | bytes accessed | tf_op | source)
XLA Modules:
  0.0 86.4 jit_solution(6967423175514840928)
XLA Ops:
  0.6 1.3 %prepared.1 = (bf16[16,2,64,128]{3,2,1,0:T(8,128)(2,1)S(1)}, f32[8,8,128]{2,1,0:T(8,128)S(1)}, f32[64,128]{1,0:T(8,128)S(1)}, bf16[64,128]{1,0:T(8,128)(2,1)S(1)}) custom-call(s32[1]{0:T(128)} %bitcast.z_ref, s32[32]{0:T(128)} %counts.1, bf16[1,262144]{1,0:T(2,128)(2,1)} %src.1, f32[64,128]{1,0:T(8,128)} %bitcast.25, bf16[64,128]{1,0:T(8,128)(2,1)} %bitcast.26), custom_call_target="tpu_custom_call" | custom-call | tf_op jit(solution)/shard_map/prepared/pallas_call | solution.py:70
  1.9 32.3 %all_to_all.10.got_ref = bf16[16,2,64,128]{3,2,1,0:T(8,128)(2,1)S(1)} all-to-all(bf16[16,2,64,128]{3,2,1,0:T(8,128)(2,1)S(1)} %get-tuple-element.11), channel_id=1, replica_groups={{0,128,64,192,32,160,96,224,16,144,80,208,48,176,112,240},{1,129,65,193..., dimensions={0} | all-to-all | bytes 1048576 | tf_op jit(solution)/shard_map/all_to_all | solution.py:148
  34.2 0.1 weighted.1
  34.3 26.0 %all-gather = f32[16,64,128]{2,1,0:T(8,128)S(1)} all-gather(f32[4,64,128]{2,1,0:T(8,128)S(1)} %get-tuple-element.14), channel_id=2, replica_groups=mesh['z'=4,'yc'=16,'shard'=16] {'z'}, dimensions={0}, use_global_device_ids=true | all-gather | bytes 655360 | tf_op jit(solution)/shard_map/all_gather | solution.py:161
  60.4 0.1 broadcast_in_dim.10
  60.5 15.3 %all_to_all.11 = bf16[8,4,64,128]{3,2,1,0:T(8,128)(2,1)S(1)} all-to-all(bf16[8,4,64,128]{3,2,1,0:T(8,128)(2,1)S(1)} %broadcast_in_dim.10), channel_id=1, replica_groups={{0,128,64,192,32,160,96,224},{16,144,80,208,48,176,112,240},{1,129,65,1..., dimensions={0} | all-to-all | bytes 1048576 | tf_op jit(solution)/shard_map/all_to_all | solution.py:148
  75.8 7.9 %collective-permute-start = (bf16[8,4,64,128]{3,2,1,0:T(8,128)(2,1)S(1)}, bf16[8,4,64,128]{3,2,1,0:T(8,128)(2,1)S(1)}, u32[]{:S(2)}, u32[]{:S(2)}) collective-permute-start(bf16[8,4,64,128]{3,2,1,0:T(8,128)(2,1)S(1)} %all_to_all.11), channel_id=1, source_target_pairs={{0,16},{16,0},{32,48},{48,32},{64,80},{80,64},{96,112},{112,96},{1... | collective-permute-start | bytes 1572872 | tf_op jit(solution)/shard_map/ppermute | solution.py:163
  83.8 0.6 copy.18
  84.4 0.2 broadcast_in_dim.4
  84.7 0.1 constant_dynamic-update-slice_fusion.1
  84.8 0.5 collective-permute-done
  85.3 0.1 constant_dynamic-update-slice_fusion
  85.4 0.0 copy-start
  85.4 1.0 %copy-done = bf16[4,8,2,64,128]{4,3,2,1,0:T(8,128)(2,1)} copy-done((bf16[4,8,2,64,128]{4,3,2,1,0:T(8,128)(2,1)}, bf16[4,8,2,64,128]{4,3,2,1,0:T(8,128)(2,1)S(1)}, u32[]{:S(2)}) %copy-start) | copy-done | bytes 1048600
  (3 shorter events, 0.1 us)
Async XLA Ops:
  75.8 9.4 %collective-permute-start = (bf16[8,4,64,128]{3,2,1,0:T(8,128)(2,1)S(1)}, bf16[8,4,64,128]{3,2,1,0:T(8,128)(2,1)S(1)}, u32[]{:S(2)}, u32[]{:S(2)}) collective-permute-start(bf16[8,4,64,128]{3,2,1,0:T(8,128)(2,1)S(1)} %all_to_all.11), channel_id=1, source_target_pairs={{0,16},{16,0},{32,48},{48,32},{64,80},{80,64},{96,112},{112,96},{1... | collective-permute-start | bytes 1572872 | tf_op jit(solution)/shard_map/ppermute | solution.py:163
  85.4 1.0 %copy-start = (bf16[4,8,2,64,128]{4,3,2,1,0:T(8,128)(2,1)}, bf16[4,8,2,64,128]{4,3,2,1,0:T(8,128)(2,1)S(1)}, u32[]{:S(2)}) copy-start(bf16[4,8,2,64,128]{4,3,2,1,0:T(8,128)(2,1)S(1)} %constant_dynamic-update-slice_fusion) | copy-start | bytes 3145732

commit v3 on v2

--- a/solution.py
+++ b/solution.py
@@ -13,7 +13,7 @@
 READS = 4
 Y_ORDER = (0, 4, 2, 6, 1, 5, 3, 7)
 CORES = 2
-ALL_ORDER = [y * CORES + c for c in range(CORES) for y in Y_ORDER]
+ALL_ORDER = [y * CORES + c for c in range(CORES) for y in Y_ORDER[:: 1 - 2 * c]]
 SAME_CORE = [[y * CORES + c for y in Y_ORDER] for c in range(CORES)]
 
 VMEM = pl.BlockSpec(memory_space=pltpu.VMEM)

time: 87.7 us -> 87.4 us (level)
  starting transfers between devices: 7.92 us -> 6.4 us
  blocking collectives: 73.6 us -> 74.6 us
    ppermute x1, starting transfers between devices: 7.92 us -> 6.4 us  [local(): other = lax.ppermute(own, 'yc', [(i, i ^ 1) for i in range(ny * nc)])]
where the time goes in v3:
time: 87.4 us; the launch traced here: 85.8 us
  blocking collectives  74.6 us (85%)
  starting transfers between devices  6.4 us (7%)
  local copies, waits for them, and re-layouts  2.15 us (2%)
  Pallas kernels  1.45 us (2%)
    all_to_all x2, blocking collectives, exchanged(): return lax.all_to_all(x, 'yc', 0, 0, tiled=True, axis_index_groups=groups)  47.8 us
    all_gather x1, blocking collectives, local(): new_momentum, plane = updated(lax.all_gather(partial, 'z'), mine, old, z)  26.8 us
    ppermute x1, starting transfers between devices, local(): other = lax.ppermute(own, 'yc', [(i, i ^ 1) for i in range(ny * nc)])  6.4 us
  transfers between devices with their start and end apart: 1, of which 1 were waited for; matrix products, arithmetic and copies ran while one was open for 1% of the time, Pallas kernels for 0%

profile of v3, /device:TPU:1, one launch (start us, length us, event | category | flops | bytes accessed | tf_op | source)
XLA Modules:
  0.0 85.8 jit_solution(11653366309036914181)
XLA Ops:
  0.6 1.3 %prepared.1 = (bf16[16,2,64,128]{3,2,1,0:T(8,128)(2,1)S(1)}, f32[8,8,128]{2,1,0:T(8,128)S(1)}, f32[64,128]{1,0:T(8,128)S(1)}, bf16[64,128]{1,0:T(8,128)(2,1)S(1)}) custom-call(s32[1]{0:T(128)} %bitcast.z_ref, s32[32]{0:T(128)} %counts.1, bf16[1,262144]{1,0:T(2,128)(2,1)} %src.1, f32[64,128]{1,0:T(8,128)} %bitcast.25, bf16[64,128]{1,0:T(8,128)(2,1)} %bitcast.26), custom_call_target="tpu_custom_call" | custom-call | tf_op jit(solution)/shard_map/prepared/pallas_call | solution.py:70
  1.9 30.3 %all_to_all.10.got_ref = bf16[16,2,64,128]{3,2,1,0:T(8,128)(2,1)S(1)} all-to-all(bf16[16,2,64,128]{3,2,1,0:T(8,128)(2,1)S(1)} %get-tuple-element.11), channel_id=1, replica_groups={{0,128,64,192,32,160,96,224,240,112,176,48,208,80,144,16},{1,129,65,193..., dimensions={0} | all-to-all | bytes 1048576 | tf_op jit(solution)/shard_map/all_to_all | solution.py:148
  32.3 0.1 weighted.1
  32.4 26.8 %all-gather = f32[16,64,128]{2,1,0:T(8,128)S(1)} all-gather(f32[4,64,128]{2,1,0:T(8,128)S(1)} %get-tuple-element.14), channel_id=2, replica_groups=mesh['z'=4,'yc'=16,'shard'=16] {'z'}, dimensions={0}, use_global_device_ids=true | all-gather | bytes 655360 | tf_op jit(solution)/shard_map/all_gather | solution.py:161
  59.2 0.1 broadcast_in_dim.10
  59.3 17.5 %all_to_all.11 = bf16[8,4,64,128]{3,2,1,0:T(8,128)(2,1)S(1)} all-to-all(bf16[8,4,64,128]{3,2,1,0:T(8,128)(2,1)S(1)} %broadcast_in_dim.10), channel_id=1, replica_groups={{0,128,64,192,32,160,96,224},{16,144,80,208,48,176,112,240},{1,129,65,1..., dimensions={0} | all-to-all | bytes 1048576 | tf_op jit(solution)/shard_map/all_to_all | solution.py:148
  76.8 6.4 %collective-permute-start = (bf16[8,4,64,128]{3,2,1,0:T(8,128)(2,1)S(1)}, bf16[8,4,64,128]{3,2,1,0:T(8,128)(2,1)S(1)}, u32[]{:S(2)}, u32[]{:S(2)}) collective-permute-start(bf16[8,4,64,128]{3,2,1,0:T(8,128)(2,1)S(1)} %all_to_all.11), channel_id=1, source_target_pairs={{0,16},{16,0},{32,48},{48,32},{64,80},{80,64},{96,112},{112,96},{1... | collective-permute-start | bytes 1572872 | tf_op jit(solution)/shard_map/ppermute | solution.py:163
  83.2 0.6 copy.18
  83.9 0.2 broadcast_in_dim.4
  84.1 0.1 constant_dynamic-update-slice_fusion.1
  84.2 0.5 collective-permute-done
  84.8 0.1 constant_dynamic-update-slice_fusion
  84.8 0.0 copy-start
  84.9 1.0 %copy-done = bf16[4,8,2,64,128]{4,3,2,1,0:T(8,128)(2,1)} copy-done((bf16[4,8,2,64,128]{4,3,2,1,0:T(8,128)(2,1)}, bf16[4,8,2,64,128]{4,3,2,1,0:T(8,128)(2,1)S(1)}, u32[]{:S(2)}) %copy-start) | copy-done | bytes 1048600
  (3 shorter events, 0.1 us)
Async XLA Ops:
  76.8 7.9 %collective-permute-start = (bf16[8,4,64,128]{3,2,1,0:T(8,128)(2,1)S(1)}, bf16[8,4,64,128]{3,2,1,0:T(8,128)(2,1)S(1)}, u32[]{:S(2)}, u32[]{:S(2)}) collective-permute-start(bf16[8,4,64,128]{3,2,1,0:T(8,128)(2,1)S(1)} %all_to_all.11), channel_id=1, source_target_pairs={{0,16},{16,0},{32,48},{48,32},{64,80},{80,64},{96,112},{112,96},{1... | collective-permute-start | bytes 1572872 | tf_op jit(solution)/shard_map/ppermute | solution.py:163
  84.8 1.0 %copy-start = (bf16[4,8,2,64,128]{4,3,2,1,0:T(8,128)(2,1)}, bf16[4,8,2,64,128]{4,3,2,1,0:T(8,128)(2,1)S(1)}, u32[]{:S(2)}) copy-start(bf16[4,8,2,64,128]{4,3,2,1,0:T(8,128)(2,1)S(1)} %constant_dynamic-update-slice_fusion) | copy-start | bytes 3145732

commit v4 on v3

--- a/solution.py
+++ b/solution.py
@@ -13,7 +13,8 @@
 READS = 4
 Y_ORDER = (0, 4, 2, 6, 1, 5, 3, 7)
 CORES = 2
-ALL_ORDER = [y * CORES + c for c in range(CORES) for y in Y_ORDER[:: 1 - 2 * c]]
+FIRST_ORDER = (0, 4, 1, 5, 2, 6, 3, 7)
+ALL_ORDER = [y * CORES + c for c in range(CORES) for y in FIRST_ORDER[:: 1 - 2 * c]]
 SAME_CORE = [[y * CORES + c for y in Y_ORDER] for c in range(CORES)]
 
 VMEM = pl.BlockSpec(memory_space=pltpu.VMEM)

time: 87.4 us -> 87.8 us (level)
  blocking collectives: 74.6 us -> 75.9 us
    all_to_all x2, blocking collectives: 47.8 us -> 50.5 us  [exchanged(): return lax.all_to_all(x, 'yc', 0, 0, tiled=True, axis_index_groups=groups)]
    all_gather x1, blocking collectives: 26.8 us -> 25.4 us  [local(): new_momentum, plane = updated(lax.all_gather(partial, 'z'), mine, old, z)]
where the time goes in v4:
time: 87.8 us; the launch traced here: 86.4 us
  blocking collectives  75.9 us (86%)
  starting transfers between devices  5.65 us (6%)
  local copies, waits for them, and re-layouts  2.15 us (2%)
  Pallas kernels  1.45 us (2%)
    all_to_all x2, blocking collectives, exchanged(): return lax.all_to_all(x, 'yc', 0, 0, tiled=True, axis_index_groups=groups)  50.5 us
    all_gather x1, blocking collectives, local(): new_momentum, plane = updated(lax.all_gather(partial, 'z'), mine, old, z)  25.4 us
    ppermute x1, starting transfers between devices, local(): other = lax.ppermute(own, 'yc', [(i, i ^ 1) for i in range(ny * nc)])  5.65 us
  transfers between devices with their start and end apart: 1, of which 1 were waited for; matrix products, arithmetic and copies ran while one was open for 1% of the time, Pallas kernels for 0%

profile of v4, /device:TPU:1, one launch (start us, length us, event | category | flops | bytes accessed | tf_op | source)
XLA Modules:
  0.0 86.4 jit_solution(2490790418714339993)
XLA Ops:
  0.6 1.3 %prepared.1 = (bf16[16,2,64,128]{3,2,1,0:T(8,128)(2,1)S(1)}, f32[8,8,128]{2,1,0:T(8,128)S(1)}, f32[64,128]{1,0:T(8,128)S(1)}, bf16[64,128]{1,0:T(8,128)(2,1)S(1)}) custom-call(s32[1]{0:T(128)} %bitcast.z_ref, s32[32]{0:T(128)} %counts.1, bf16[1,262144]{1,0:T(2,128)(2,1)} %src.1, f32[64,128]{1,0:T(8,128)} %bitcast.25, bf16[64,128]{1,0:T(8,128)(2,1)} %bitcast.26), custom_call_target="tpu_custom_call" | custom-call | tf_op jit(solution)/shard_map/prepared/pallas_call | solution.py:71
  1.9 30.8 %all_to_all.10.got_ref = bf16[16,2,64,128]{3,2,1,0:T(8,128)(2,1)S(1)} all-to-all(bf16[16,2,64,128]{3,2,1,0:T(8,128)(2,1)S(1)} %get-tuple-element.11), channel_id=1, replica_groups={{0,128,32,160,64,192,96,224,240,112,208,80,176,48,144,16},{1,129,33,161..., dimensions={0} | all-to-all | bytes 1048576 | tf_op jit(solution)/shard_map/all_to_all | solution.py:149
  32.8 0.1 weighted.1
  32.9 25.4 %all-gather = f32[16,64,128]{2,1,0:T(8,128)S(1)} all-gather(f32[4,64,128]{2,1,0:T(8,128)S(1)} %get-tuple-element.14), channel_id=2, replica_groups=mesh['z'=4,'yc'=16,'shard'=16] {'z'}, dimensions={0}, use_global_device_ids=true | all-gather | bytes 655360 | tf_op jit(solution)/shard_map/all_gather | solution.py:162
  58.3 0.1 broadcast_in_dim.10
  58.4 19.7 %all_to_all.11 = bf16[8,4,64,128]{3,2,1,0:T(8,128)(2,1)S(1)} all-to-all(bf16[8,4,64,128]{3,2,1,0:T(8,128)(2,1)S(1)} %broadcast_in_dim.10), channel_id=1, replica_groups={{0,128,64,192,32,160,96,224},{16,144,80,208,48,176,112,240},{1,129,65,1..., dimensions={0} | all-to-all | bytes 1048576 | tf_op jit(solution)/shard_map/all_to_all | solution.py:149
  78.1 5.6 %collective-permute-start = (bf16[8,4,64,128]{3,2,1,0:T(8,128)(2,1)S(1)}, bf16[8,4,64,128]{3,2,1,0:T(8,128)(2,1)S(1)}, u32[]{:S(2)}, u32[]{:S(2)}) collective-permute-start(bf16[8,4,64,128]{3,2,1,0:T(8,128)(2,1)S(1)} %all_to_all.11), channel_id=1, source_target_pairs={{0,16},{16,0},{32,48},{48,32},{64,80},{80,64},{96,112},{112,96},{1... | collective-permute-start | bytes 1572872 | tf_op jit(solution)/shard_map/ppermute | solution.py:164
  83.8 0.6 copy.18
  84.5 0.2 broadcast_in_dim.4
  84.7 0.1 constant_dynamic-update-slice_fusion.1
  84.8 0.5 collective-permute-done
  85.3 0.1 constant_dynamic-update-slice_fusion
  85.4 0.0 copy-start
  85.4 1.0 %copy-done = bf16[4,8,2,64,128]{4,3,2,1,0:T(8,128)(2,1)} copy-done((bf16[4,8,2,64,128]{4,3,2,1,0:T(8,128)(2,1)}, bf16[4,8,2,64,128]{4,3,2,1,0:T(8,128)(2,1)S(1)}, u32[]{:S(2)}) %copy-start) | copy-done | bytes 1048600
  (3 shorter events, 0.1 us)
Async XLA Ops:
  78.1 7.2 %collective-permute-start = (bf16[8,4,64,128]{3,2,1,0:T(8,128)(2,1)S(1)}, bf16[8,4,64,128]{3,2,1,0:T(8,128)(2,1)S(1)}, u32[]{:S(2)}, u32[]{:S(2)}) collective-permute-start(bf16[8,4,64,128]{3,2,1,0:T(8,128)(2,1)S(1)} %all_to_all.11), channel_id=1, source_target_pairs={{0,16},{16,0},{32,48},{48,32},{64,80},{80,64},{96,112},{112,96},{1... | collective-permute-start | bytes 1572872 | tf_op jit(solution)/shard_map/ppermute | solution.py:164
  85.4 1.0 %copy-start = (bf16[4,8,2,64,128]{4,3,2,1,0:T(8,128)(2,1)}, bf16[4,8,2,64,128]{4,3,2,1,0:T(8,128)(2,1)S(1)}, u32[]{:S(2)}) copy-start(bf16[4,8,2,64,128]{4,3,2,1,0:T(8,128)(2,1)S(1)} %constant_dynamic-update-slice_fusion) | copy-start | bytes 3145732
